TPU v7x, 32 devices: a whole 2x2x4 slice. The times are simulated.
32 devices in a mesh: col: 4 (over z), row: 8 (over y, x, core).
Axes of the slice: x: 2, y: 2, z: 4, core: 2. Of those that a mesh axis runs over, the one named last changes fastest.
Arguments:
- inter_mask: int32 [4096, 65536], P('row', 'col')
- emb_user: bfloat16 [4096, 32], P(('row', 'col'))
- emb_item: bfloat16 [65536, 32], P(('col', 'row'))
- triples: int32 [4096, 3], replicated
Outputs:
- output 1: bfloat16 [4096, 32], P(('row', 'col'))
- output 2: bfloat16 [65536, 32], P(('col', 'row'))
- output 3: float32 [4096], replicated
All inputs are finite; a program needn't handle non-finite values.
Results may differ from a plain program's by a relative error of at most 0.00855594.
Values are sent between devices in bfloat16 or wider.
A program may use at most 1 GiB of HBM per device.

v0:
```python
import jax
import jax.numpy as jnp
from jax import lax
from jax.sharding import PartitionSpec as P

LAYERS = 3


def solution(mesh):
    row_count = mesh.shape["row"]
    col_count = mesh.shape["col"]

    def lookup(emb_table, row_ids, row_start):
        local_ids = row_ids - row_start
        is_owned = (local_ids >= 0) & (local_ids < emb_table.shape[0])
        rows_got = jnp.take(emb_table, jnp.clip(local_ids, 0, emb_table.shape[0] - 1), axis=0).astype(jnp.float32)
        return jnp.where(is_owned[:, None], rows_got, 0.0)

    def device_body(mask_blk, user_shard, item_shard, triples):
        row_idx = lax.axis_index("row")
        col_idx = lax.axis_index("col")
        deg_user = lax.psum(jnp.sum(mask_blk, axis=1), "col")
        deg_item = lax.psum(jnp.sum(mask_blk, axis=0), "row")
        scale_user = lax.rsqrt(jnp.maximum(deg_user, 1).astype(jnp.float32))
        scale_item = lax.rsqrt(jnp.maximum(deg_item, 1).astype(jnp.float32))
        adj_norm = (mask_blk.astype(jnp.float32) * scale_user[:, None] * scale_item[None, :]).astype(jnp.bfloat16)
        cur_user = user_shard
        cur_item = item_shard
        total_user = user_shard.astype(jnp.float32)
        total_item = item_shard.astype(jnp.float32)
        for layer_idx in range(LAYERS):
            item_panel = lax.all_gather(cur_item, "row", axis=0, tiled=True)
            user_panel = lax.all_gather(cur_user, "col", axis=0, tiled=True)
            user_part = jnp.dot(adj_norm, item_panel, preferred_element_type=jnp.float32)
            item_part = jnp.einsum("ui,ud->id", adj_norm, user_panel, preferred_element_type=jnp.float32)
            cur_user = lax.psum_scatter(user_part, "col", scatter_dimension=0, tiled=True).astype(jnp.bfloat16)
            cur_item = lax.psum_scatter(item_part, "row", scatter_dimension=0, tiled=True).astype(jnp.bfloat16)
            total_user = total_user + cur_user.astype(jnp.float32)
            total_item = total_item + cur_item.astype(jnp.float32)
        out_user = (total_user / (LAYERS + 1)).astype(jnp.bfloat16)
        out_item = (total_item / (LAYERS + 1)).astype(jnp.bfloat16)
        user_start = (row_idx * col_count + col_idx) * out_user.shape[0]
        item_start = (col_idx * row_count + row_idx) * out_item.shape[0]
        picked = jnp.concatenate([
            lookup(out_user, triples[:, 0], user_start),
            lookup(out_item, triples[:, 1], item_start),
            lookup(out_item, triples[:, 2], item_start),
        ], axis=0)
        picked = lax.psum(picked, ("row", "col"))
        batch_n = triples.shape[0]
        vec_user = picked[:batch_n]
        vec_pos = picked[batch_n:2 * batch_n]
        vec_neg = picked[2 * batch_n:]
        margin = jnp.sum(vec_user * vec_pos, axis=1) - jnp.sum(vec_user * vec_neg, axis=1)
        bpr_loss = jax.nn.softplus(-margin)
        return out_user, out_item, bpr_loss

    return jax.shard_map(
        device_body,
        mesh=mesh,
        in_specs=(P("row", "col"), P(("row", "col"), None), P(("col", "row"), None), P()),
        out_specs=(P(("row", "col"), None), P(("col", "row"), None), P()),
        check_vma=False,
    )
```

profile of v0, /device:TPU:0, one launch (start us, length us, event | category | flops | bytes accessed | tf_op | source)
XLA Modules:
  0.0 525.2 jit_solution(2113496981387403879)
XLA Ops:
  7.2 0.0 all-reduce.3.cloned.1.call-start
  7.2 13.1 %fusion.4 = (s32[512]{0:T(512)S(1)}, s32[16384]{0:T(1024)}) fusion(s32[512,16384]{1,0:T(8,128)} %param.6), kind=kLoop, calls=%fused_computation.34 | loop fusion | flops 16760320 | bytes 33622016 | tf_op jit(solution)/shard_map/reduce_sum | solution.py:22
  20.3 0.0 all-reduce.3.cloned.1.call-update
  20.4 0.0 all-gather.4.cloned.1.call-start
  20.4 0.7 all-gather.4.cloned.1.call-update
  21.1 0.0 reduce-scatter.9.cloned.1.call-start
  21.2 10.0 %psum.21 = s32[512]{0:T(512)S(1)} all-reduce(s32[512]{0:T(512)S(1)} %get-tuple-element.4), channel_id=1, replica_groups=mesh['col'=4,'row'=8] {'col'}, use_global_device_ids=true, to_apply=%region_1.0 | all-reduce | flops 512 | bytes 4096 | tf_op jit(solution)/shard_map/psum | solution.py:22
  31.2 13.1 %all_gather.19 = bf16[512,32]{0,1:T(8,128)(2,1)S(1)} all-gather(bf16[128,32]{0,1:T(8,128)(2,1)S(1)} %copy-done.7), channel_id=1, replica_groups=mesh['col'=4,'row'=8] {'col'}, dimensions={0}, use_global_device_ids=true | all-gather | bytes 40960 | tf_op jit(solution)/shard_map/all_gather | solution.py:33
  44.3 32.0 %all-reduce.3.cloned.1.call-done = s32[16384]{0:T(1024)} async-done(((s32[16384]{0:T(1024)}), s32[16384]{0:T(1024)}) %all-reduce.3.cloned.1.call-update) | async-done | bytes 65552 | tf_op jit(solution)/shard_map/psum | solution.py:23
  76.3 0.9 convert_rsqrt_fusion
  77.2 13.1 %multiply_convert_fusion = bf16[512,16384]{1,0:T(8,128)(2,1)S(1)} fusion(s32[512,16384]{1,0:T(8,128)} %param.6, f32[16384]{0:T(1024)S(1)} %convert_rsqrt_fusion, f32[512]{0:T(512)S(1)} %convert_rsqrt_fusion.1), kind=kLoop, calls=%fused_computation.3 | loop fusion | flops 33554432 | bytes 50399232 | tf_op jit(solution)/shard_map/convert_element_type | solution.py:26
  90.3 5.7 %copy-done = bf16[512,16384]{1,0:T(8,128)(2,1)} copy-done((bf16[512,16384]{1,0:T(8,128)(2,1)}, bf16[512,16384]{1,0:T(8,128)(2,1)S(1)}, u32[]{:S(2)}) %copy-start) | copy-done | bytes 16777240
  96.0 4.3 fusion.8
  100.4 0.0 reduce-scatter.9.cloned.1.call-update
  100.4 0.0 reduce-scatter.7.cloned.1.call-start
  100.4 0.3 all-gather.4.cloned.1.call-done
  100.7 11.7 %fusion.5 = f32[512,32]{0,1:T(8,128)} fusion(bf16[512,16384]{1,0:T(8,128)(2,1)} %copy-done, bf16[16384,32]{0,1:T(8,128)(2,1)} %all-gather.4.cloned.1.call-done), kind=kOutput, calls=%fused_computation.35 | convolution fusion | flops 536870912 | bytes 17891328 | tf_op jit(solution)/shard_map/dot_general | solution.py:34
  112.5 0.0 reduce-scatter.7.cloned.1.call-update
  112.5 0.0 all-gather.6.cloned.1.call-start
  112.5 32.4 %reduce-scatter.9.cloned.1.call-done = f32[2048,32]{0,1:T(8,128)} async-done(((f32[16384,32]{0,1:T(8,128)}), f32[2048,32]{0,1:T(8,128)}) %reduce-scatter.9.cloned.1.call-update) | async-done | bytes 262160 | tf_op jit(solution)/shard_map/reduce_scatter | solution.py:37
  145.0 1.6 convert_element_type.76
  146.6 0.0 all-gather.6.cloned.1.call-update
  146.6 0.0 reduce-scatter.11.cloned.1.call-start
  146.7 19.7 %reduce-scatter.7.cloned.1.call-done = f32[128,32]{0,1:T(8,128)} async-done(((f32[512,32]{0,1:T(8,128)}), f32[128,32]{0,1:T(8,128)}) %reduce-scatter.7.cloned.1.call-update) | async-done | bytes 16400 | tf_op jit(solution)/shard_map/reduce_scatter | solution.py:36
  166.4 0.7 convert_element_type.74
  167.1 13.3 %all_gather.21 = bf16[512,32]{0,1:T(8,128)(2,1)S(1)} all-gather(bf16[128,32]{0,1:T(8,128)(2,1)S(1)} %convert_element_type.74), channel_id=1, replica_groups=mesh['col'=4,'row'=8] {'col'}, dimensions={0}, use_global_device_ids=true | all-gather | bytes 40960 | tf_op jit(solution)/shard_map/all_gather | solution.py:33
  180.3 9.7 %all-gather.6.cloned.1.call-done = bf16[16384,32]{0,1:T(8,128)(2,1)} async-done(((bf16[2048,32]{0,1:T(8,128)(2,1)}), bf16[16384,32]{0,1:T(8,128)(2,1)}) %all-gather.6.cloned.1.call-update) | async-done | bytes 1048592 | tf_op jit(solution)/shard_map/all_gather | solution.py:32
  190.0 11.7 %fusion.6 = f32[512,32]{0,1:T(8,128)} fusion(bf16[512,16384]{1,0:T(8,128)(2,1)} %copy-done, bf16[16384,32]{0,1:T(8,128)(2,1)} %all-gather.6.cloned.1.call-done), kind=kOutput, calls=%fused_computation.36 | convolution fusion | flops 536870912 | bytes 17891328 | tf_op jit(solution)/shard_map/dot_general | solution.py:34
  201.7 0.0 reduce-scatter.11.cloned.1.call-update
  201.8 0.0 reduce-scatter.13.cloned.1.call-start
  201.8 10.2 %fusion.9 = f32[16384,32]{0,1:T(8,128)} fusion(bf16[512,32]{0,1:T(8,128)(2,1)S(1)} %all_gather.21, bf16[512,16384]{1,0:T(8,128)(2,1)} %copy-done), kind=kOutput, calls=%fused_computation.39 | convolution fusion | flops 536870912 | bytes 18907136 | tf_op jit(solution)/shard_map/ui,ud->id/dot_general | solution.py:35
  212.0 0.0 reduce-scatter.13.cloned.1.call-update
  212.0 0.0 reduce-scatter.17.cloned.1.call-start
  212.1 9.1 %reduce-scatter.11.cloned.1.call-done = f32[128,32]{0,1:T(8,128)} async-done(((f32[512,32]{0,1:T(8,128)}), f32[128,32]{0,1:T(8,128)}) %reduce-scatter.11.cloned.1.call-update) | async-done | bytes 16400 | tf_op jit(solution)/shard_map/reduce_scatter | solution.py:36
  221.2 0.7 convert_element_type.77
  221.9 13.1 %all_gather.23 = bf16[512,32]{0,1:T(8,128)(2,1)S(1)} all-gather(bf16[128,32]{0,1:T(8,128)(2,1)S(1)} %convert_element_type.77), channel_id=1, replica_groups=mesh['col'=4,'row'=8] {'col'}, dimensions={0}, use_global_device_ids=true | all-gather | bytes 40960 | tf_op jit(solution)/shard_map/all_gather | solution.py:33
  235.0 10.1 %fusion.10 = f32[16384,32]{0,1:T(8,128)} fusion(bf16[512,32]{0,1:T(8,128)(2,1)S(1)} %all_gather.23, bf16[512,16384]{1,0:T(8,128)(2,1)} %copy-done), kind=kOutput, calls=%fused_computation.40 | convolution fusion | flops 536870912 | bytes 18907136 | tf_op jit(solution)/shard_map/ui,ud->id/dot_general | solution.py:35
  245.0 0.0 reduce-scatter.17.cloned.1.call-update
  245.1 0.0 all-gather.8.cloned.1.call-start
  245.1 18.5 %reduce-scatter.13.cloned.1.call-done = f32[2048,32]{0,1:T(8,128)} async-done(((f32[16384,32]{0,1:T(8,128)}), f32[2048,32]{0,1:T(8,128)}) %reduce-scatter.13.cloned.1.call-update) | async-done | bytes 262160 | tf_op jit(solution)/shard_map/reduce_scatter | solution.py:37
  263.6 44.2 %reduce-scatter.17.cloned.1.call-done = f32[2048,32]{0,1:T(8,128)} async-done(((f32[16384,32]{0,1:T(8,128)}), f32[2048,32]{0,1:T(8,128)}) %reduce-scatter.17.cloned.1.call-update) | async-done | bytes 262160 | tf_op jit(solution)/shard_map/reduce_scatter | solution.py:37
  307.9 1.7 multiply_convert_fusion.1
  309.6 0.3 reduce-scatter.15.cloned.1.call-start
  309.9 0.1 broadcast_clamp_fusion.2
  310.0 0.3 and_reduce_fusion.2
  310.3 0.3 copy.11
  310.6 12.1 %gather_fusion.2 = bf16[4096,32]{1,0:T(8,128)(2,1)S(1)} fusion(bf16[2048,32]{1,0:T(8,128)(2,1)S(1)} %copy.11, s32[4096]{0:T(1024)S(1)} %fusion.3), kind=kCustom, calls=%fused_computation.1.clone | custom fusion | bytes 540672 | tf_op jit(solution)/shard_map/jit(_take)/gather | solution.py:16
  322.8 14.9 %gather_fusion.1 = bf16[4096,32]{1,0:T(8,128)(2,1)} fusion(bf16[2048,32]{1,0:T(8,128)(2,1)S(1)} %copy.11, s32[4096]{0:T(1024)S(1)} %fusion.2), kind=kCustom, calls=%fused_computation.clone | custom fusion | bytes 540672 | tf_op jit(solution)/shard_map/jit(_take)/gather | solution.py:16
  337.7 11.8 %fusion.7 = f32[512,32]{0,1:T(8,128)} fusion(bf16[512,16384]{1,0:T(8,128)(2,1)} %copy-done, bf16[16384,32]{0,1:T(8,128)(2,1)} %all-gather.8.cloned.1.call-done), kind=kOutput, calls=%fused_computation.37 | convolution fusion | flops 536870912 | bytes 17891328 | tf_op jit(solution)/shard_map/dot_general | solution.py:34
  349.4 0.0 reduce-scatter.15.cloned.1.call-update
  349.5 0.0 all-reduce.5.cloned.1.call-start
  349.5 7.0 %convert_select_fusion = (f32[4096,32]{1,0:T(8,128)}, f32[4096,32]{1,0:T(8,128)S(1)}) fusion(bf16[4096,32]{1,0:T(8,128)(2,1)S(1)} %gather_fusion.2, pred[4096]{0:T(1024)(128)(4,1)S(1)} %compare_and_fusion, pred[4096]{0:T(1024)(128)(4,1)S(1)} %get-tuple-element.16, bf16[4096,32]{1,0:T(8,128)(2,1)} %gather_fusion.1, pred[4096]{0:T(1024)(128)(4,1)S(1)} %compare_and_fusion.1, ...), kind=kLoop, calls=%fused_computation.4 | loop fusion | flops 786432 | bytes 1589248 | tf_op jit(solution)/shard_map/jit(_where)/select_n | solution.py:17
  356.5 3.0 copy.15
  359.5 1.4 copy.14
  360.9 8.0 %reduce-scatter.15.cloned.1.call-done = f32[128,32]{0,1:T(8,128)} async-done(((f32[512,32]{0,1:T(8,128)}), f32[128,32]{0,1:T(8,128)}) %reduce-scatter.15.cloned.1.call-update) | async-done | bytes 16400 | tf_op jit(solution)/shard_map/reduce_scatter | solution.py:36
  368.9 0.7 multiply_convert_fusion.2
  369.6 0.1 copy.10
  369.8 12.1 %gather_fusion = bf16[4096,32]{1,0:T(8,128)(2,1)S(1)} fusion(bf16[128,32]{1,0:T(8,128)(2,1)S(1)} %copy.10, s32[4096]{0:T(1024)S(1)} %broadcast_clamp_fusion), kind=kCustom, calls=%fused_computation.2 | custom fusion | bytes 540672 | tf_op jit(solution)/shard_map/jit(_take)/gather | solution.py:16
  381.9 1.3 convert_select_fusion.2
  383.2 0.6 copy.13
  383.7 2.5 pad_maximum_fusion
  386.2 130.3 %all-reduce.5.cloned.1.call-done = f32[12288,32]{0,1:T(8,128)} async-done(((f32[12288,32]{0,1:T(8,128)}), f32[12288,32]{0,1:T(8,128)}) %all-reduce.5.cloned.1.call-update) | async-done | bytes 1572880 | tf_op jit(solution)/shard_map/psum | solution.py:49
  516.5 1.5 fusion
  518.1 0.6 compare_select_fusion.3
  (26 shorter events, 0.1 us)
Async XLA Ops:
  7.2 24.0 %copy-start.7 = (bf16[128,32]{0,1:T(8,128)(2,1)S(1)}, bf16[128,32]{0,1:T(8,128)(2,1)}, u32[]{:S(2)}) copy-start(bf16[128,32]{0,1:T(8,128)(2,1)} %param.7) | copy-start | bytes 24580
  7.2 69.1 %all-reduce.3.cloned.1.call-start = ((), (), s32[]{:S(2)}) async-start(), calls=%async_computation.6 | async-start | bytes 131072 | tf_op jit(solution)/shard_map/psum | solution.py:23
  20.4 80.4 %all-gather.4.cloned.1.call-start = ((), (), s32[]{:S(2)}) async-start(), calls=%async_computation.7 | async-start | bytes 1179648 | tf_op jit(solution)/shard_map/all_gather | solution.py:32
  21.1 123.9 %reduce-scatter.9.cloned.1.call-start = ((), (), s32[]{:S(2)}) async-start(), calls=%async_computation.9 | async-start | bytes 2359296 | tf_op jit(solution)/shard_map/reduce_scatter | solution.py:37
  90.3 5.7 %copy-start = (bf16[512,16384]{1,0:T(8,128)(2,1)}, bf16[512,16384]{1,0:T(8,128)(2,1)S(1)}, u32[]{:S(2)}) copy-start(bf16[512,16384]{1,0:T(8,128)(2,1)S(1)} %multiply_convert_fusion) | copy-start | bytes 50331652
  100.4 66.0 %reduce-scatter.7.cloned.1.call-start = ((), (), s32[]{:S(2)}) async-start(), calls=%async_computation.8 | async-start | bytes 81920 | tf_op jit(solution)/shard_map/reduce_scatter | solution.py:36
  112.5 77.5 %all-gather.6.cloned.1.call-start = ((), (), s32[]{:S(2)}) async-start(), calls=%async_computation.10 | async-start | bytes 1179648 | tf_op jit(solution)/shard_map/all_gather | solution.py:32
  146.6 74.6 %reduce-scatter.11.cloned.1.call-start = ((), (), s32[]{:S(2)}) async-start(), calls=%async_computation.11 | async-start | bytes 81920 | tf_op jit(solution)/shard_map/reduce_scatter | solution.py:36
  201.8 106.1 %copy-start.1 = (f32[2048,32]{0,1:T(8,128)S(1)}, f32[2048,32]{0,1:T(8,128)}, u32[]{:S(2)}) copy-start(f32[2048,32]{0,1:T(8,128)} %reduce-scatter.9.cloned.1.call-done) | copy-start | bytes 786436
  201.8 106.1 %copy-start.3 = (bf16[2048,32]{0,1:T(8,128)(2,1)S(1)}, bf16[2048,32]{0,1:T(8,128)(2,1)}, u32[]{:S(2)}) copy-start(bf16[2048,32]{0,1:T(8,128)(2,1)} %param.8) | copy-start | bytes 393220
  201.8 61.8 %reduce-scatter.13.cloned.1.call-start = ((), (), s32[]{:S(2)}) async-start(), calls=%async_computation.12 | async-start | bytes 2359296 | tf_op jit(solution)/shard_map/reduce_scatter | solution.py:37
  212.0 97.9 %copy-start.4 = (s32[4096,3]{0,1:T(4,128)S(1)}, s32[4096,3]{0,1:T(4,128)}, u32[]{:S(2)}) copy-start(s32[4096,3]{0,1:T(4,128)} %param.9) | copy-start | bytes 147460
  212.0 95.8 %reduce-scatter.17.cloned.1.call-start = ((), (), s32[]{:S(2)}) async-start(), calls=%async_computation.15 | async-start | bytes 2359296 | tf_op jit(solution)/shard_map/reduce_scatter | solution.py:37
  245.1 92.6 %all-gather.8.cloned.1.call-start = ((), (), s32[]{:S(2)}) async-start(), calls=%async_computation.13 | async-start | bytes 1179648 | tf_op jit(solution)/shard_map/all_gather | solution.py:32
  309.6 39.8 %copy-start.2 = (bf16[2048,32]{0,1:T(8,128)(2,1)}, bf16[2048,32]{0,1:T(8,128)(2,1)S(1)}, u32[]{:S(2)}) copy-start(bf16[2048,32]{0,1:T(8,128)(2,1)S(1)} %get-tuple-element.13) | copy-start | bytes 393220
  309.6 59.3 %reduce-scatter.15.cloned.1.call-start = ((), (), s32[]{:S(2)}) async-start(), calls=%async_computation.14 | async-start | bytes 81920 | tf_op jit(solution)/shard_map/reduce_scatter | solution.py:36
  337.7 31.2 %copy-start.5 = (f32[128,32]{0,1:T(8,128)S(1)}, f32[128,32]{0,1:T(8,128)}, u32[]{:S(2)}) copy-start(f32[128,32]{0,1:T(8,128)} %reduce-scatter.7.cloned.1.call-done) | copy-start | bytes 49156
  337.7 31.2 %copy-start.6 = (f32[128,32]{0,1:T(8,128)S(1)}, f32[128,32]{0,1:T(8,128)}, u32[]{:S(2)}) copy-start(f32[128,32]{0,1:T(8,128)} %reduce-scatter.11.cloned.1.call-done) | copy-start | bytes 49156
  349.5 167.1 %all-reduce.5.cloned.1.call-start = ((), (), s32[]{:S(2)}) async-start(), calls=%async_computation.16 | async-start | bytes 3145728 | tf_op jit(solution)/shard_map/psum | solution.py:49
  369.6 149.1 %copy-start.8 = (bf16[128,32]{0,1:T(8,128)(2,1)}, bf16[128,32]{0,1:T(8,128)(2,1)S(1)}, u32[]{:S(2)}) copy-start(bf16[128,32]{0,1:T(8,128)(2,1)S(1)} %multiply_convert_fusion.2) | copy-start | bytes 24580
Sparse Core Ops, SparseCore 0:
  20.5 55.7 all-reduce.2
  78.2 22.4 all-gather.3
  104.0 40.9 reduce-scatter.8
  147.1 19.2 reduce-scatter.6
  168.7 21.2 all-gather.5
  201.9 19.2 reduce-scatter.10
  224.5 39.1 reduce-scatter.12
  266.9 40.9 reduce-scatter.16
  309.8 23.0 all-gather.7
  349.6 19.2 reduce-scatter.14
  386.3 130.1 all-reduce.4
where the time goes:
time: 526 us; the launch traced here: 525 us
  waiting for transfers between devices  305 us (58%)
  matrix products  59.8 us (11%)
  local copies, waits for them, and re-layouts  50.3 us (10%)
  blocking collectives  49.4 us (9%)
  other arithmetic  45.9 us (9%)
  between operations  14 us (3%)
    psum x1, waiting for transfers between devices, device_body(): picked = lax.psum(picked, ('row', 'col'))  130 us
    reduce_scatter x3, waiting for transfers between devices, device_body(): lax.psum_scatter(item_part, 'row', scatter_dimension=0, tiled=True)  95.2 us
    all_gather x3, blocking collectives, device_body(): user_panel = lax.all_gather(cur_user, 'col', axis=0, tiled=True)  39.4 us
    gather x3, local copies, waits for them, and re-layouts, lookup(): jnp.take(emb_table, jnp.clip(local_ids, 0, emb_table.shape[0] - 1), axis=0)  39.2 us
    reduce_scatter x3, waiting for transfers between devices, device_body(): lax.psum_scatter(user_part, 'col', scatter_dimension=0, tiled=True)  36.8 us
    dot_general x3, matrix products, device_body(): jnp.dot(adj_norm, item_panel, preferred_element_type=jnp.float32)  35.2 us
    psum x1, waiting for transfers between devices, device_body(): deg_item = lax.psum(jnp.sum(mask_blk, axis=0), 'row')  32 us
    dot_general x3, matrix products, device_body(): jnp.einsum('ui,ud->id', adj_norm, user_panel, preferred_element_type=jnp....  24.5 us
  transfers between devices with their start and end apart: 11, of which 10 were waited for; matrix products, arithmetic and copies ran while one was open for 18% of the time, Pallas kernels for 0%

commit v1 on v0

v1 whole, which is shorter than its diff:
```python
import functools

import jax
import jax.numpy as jnp
from jax import lax
from jax.experimental import pallas as pl
from jax.experimental.pallas import tpu as pltpu
from jax.sharding import PartitionSpec as P

LAYERS = 3
ROWS = 8
COLS = 4
SLOTS = 4
CHUNKS = 16
STRIP = 32
MESH_ID = pl.DeviceIdType.MESH
F32 = jnp.float32
BF16 = jnp.bfloat16

DEG = 0
UDEG = 28
AG = 31
ZAG = AG + 21
ZRS = ZAG + 9
RS_D = ZRS + 9
RS_1 = RS_D + 12
RS_2 = RS_1 + 12
OUZ = RS_2 + 6
OUR = OUZ + 3
MGZ = OUR + 7
MGR = MGZ + 3
N_SEM = MGR + 7


def nt_dot(a, b):
    return lax.dot_general(a, b, (((1,), (1,)), ((), ())), preferred_element_type=F32)


def kernel(mask_hbm, eu_ref, ei_ref, ids_ref, outu_ref, outi_ref, margin_ref,
           a_ref, mbuf, deg_own, deg_in, deg_inv, udeg_part, udeg_own, udeg_in, su_ref,
           part, d_in, r1_in, r2_in, eig, eug, pu, pu_in, tot_i, tot_u,
           items_lo, ug, u_rows, mg, mg_z, mg_zsum, mg_r,
           copy_sem, send_sem, recv_sem):
    emb, seg = ei_ref.shape
    users, block = a_ref.shape
    ush = eu_ref.shape[1]
    cw = block // CHUNKS
    dw = block // 32
    row = lax.axis_index("row")
    col = lax.axis_index("col")
    core = lax.rem(row, 2)
    quad = row // 2
    partner = row + 1 - 2 * core
    xq = quad + 1 - 2 * lax.rem(quad, 2)
    yq = lax.rem(quad + 2, 4)
    dq = 3 - quad
    x_row, y_row, d_row = 2 * xq + core, 2 * yq + core, 2 * dq + core
    chip_rows = (x_row, y_row, d_row)
    half = emb // 2
    sent = []

    def remote(src, dst, idx, **where):
        return pltpu.make_async_remote_copy(
            src_ref=src, dst_ref=dst, send_sem=send_sem.at[idx], recv_sem=recv_sem.at[idx],
            device_id=where, device_id_type=MESH_ID)

    def send(src, dst, idx, **where):
        copy = remote(src, dst, idx, **where)
        copy.start()
        sent.append(copy)

    def arrived(dst, idx):
        remote(dst, dst, idx, row=row).wait_recv()

    def mask_copy(j):
        return pltpu.make_async_copy(
            mask_hbm.at[:, pl.ds(j * cw, cw)], mbuf.at[j % SLOTS], copy_sem.at[j % SLOTS])

    for j in range(SLOTS):
        mask_copy(j).start()

    barrier = pltpu.get_barrier_semaphore()
    for k in range(1, ROWS):
        pl.semaphore_signal(barrier, inc=1, device_id={"row": lax.rem(row + k, ROWS)}, device_id_type=MESH_ID)
    for k in range(1, COLS):
        pl.semaphore_signal(barrier, inc=1, device_id={"col": lax.rem(col + k, COLS)}, device_id_type=MESH_ID)
    pl.semaphore_wait(barrier, ROWS + COLS - 2)

    def items_out(layer, src):
        for k in range(3):
            send(src, eig.at[layer, row], AG + 7 * layer + k, row=chip_rows[k])
        send(src, eig.at[layer, row], AG + 7 * layer + 3, row=partner)

    def items_forward(layer):
        for k in range(3):
            ref = eig.at[layer, chip_rows[k]]
            arrived(ref, AG + 7 * layer + k)
            send(ref, ref, AG + 7 * layer + 4 + k, row=partner)

    def items_in(layer):
        for k in range(4):
            arrived(eig.at[layer, 0], AG + 7 * layer + 3 + k)

    def users_out(layer, src):
        for k in range(1, COLS):
            send(src, eug.at[layer, col], ZAG + 3 * layer + k - 1, col=lax.rem(col + k, COLS))

    def users_in(layer):
        for k in range(COLS - 1):
            arrived(eug.at[layer, 0], ZAG + 3 * layer + k)

    eug[0, col] = eu_ref[...]
    eig[0, row] = ei_ref[...]
    users_out(0, eu_ref)
    items_out(0, ei_ref)

    udeg_part[...] = jnp.zeros_like(udeg_part)
    for j in range(CHUNKS):
        mask_copy(j).wait()

        def strip(s, acc, j=j):
            rows = pl.ds(pl.multiple_of(s * STRIP, STRIP), STRIP)
            m = mbuf[j % SLOTS, rows, :].astype(F32)
            a_ref[rows, j * cw:(j + 1) * cw] = m.astype(BF16)
            lanes = m[:, 0:128]
            for t in range(1, cw // 128):
                lanes = lanes + m[:, t * 128:(t + 1) * 128]
            udeg_part[rows, :] = udeg_part[rows, :] + lanes
            for t in range(STRIP // 8):
                acc = acc + m[t * 8:(t + 1) * 8, :]
            return acc

        acc = lax.fori_loop(0, users // STRIP, strip, jnp.zeros((8, cw), F32))
        if j + SLOTS < CHUNKS:
            mask_copy(j + SLOTS).start()
        total = jnp.sum(acc, axis=0, keepdims=True)
        deg_own[2 * j:2 * j + 1, :] = total[:, :dw]
        deg_own[2 * j + 1:2 * j + 2, :] = total[:, dw:]
        if j % 4 == 3:
            g = j // 4
            for k in range(1, ROWS):
                send(deg_own.at[pl.ds(8 * g, 8), :], deg_in.at[k, pl.ds(8 * g, 8), :],
                     DEG + 7 * g + k - 1, row=lax.rem(row + k, ROWS))
        if j == 7:
            items_forward(0)

    udeg_own[...] = nt_dot(jnp.ones((8, 128), BF16), udeg_part[...].astype(BF16))
    for k in range(1, COLS):
        send(udeg_own, udeg_in.at[k], UDEG + k - 1, col=lax.rem(col + k, COLS))
    users_in(0)
    items_in(0)
    for k in range(1, COLS):
        arrived(udeg_in.at[k], UDEG + k - 1)
    du = udeg_own[...] + udeg_in[1] + udeg_in[2] + udeg_in[3]
    su = lax.rsqrt(jnp.maximum(du, 1.0))
    for b in range(users // 128):
        wide = jnp.broadcast_to(su[0:1, b * 128:(b + 1) * 128], (128, 128))
        su_ref[b * 128:(b + 1) * 128, :] = wide.T
    for g in range(4):
        for k in range(1, ROWS):
            arrived(deg_in.at[k, pl.ds(8 * g, 8), :], DEG + 7 * g + k - 1)
    di = deg_own[...]
    for k in range(1, ROWS):
        di = di + deg_in[k]
    deg_inv[...] = lax.rsqrt(jnp.maximum(di, 1.0))

    def users_all(layer):
        return jnp.concatenate([eug[layer, c] for c in range(COLS)], axis=1)

    def seg_lanes(s, h=0, width=None):
        return pl.ds(pl.multiple_of(s * seg + h * cw, 128), width or seg)

    def item_dot(layer, s, eu_all):
        for h in range(2):
            part[layer, s, :, h * cw:(h + 1) * cw] = jnp.dot(
                eu_all, a_ref[:, seg_lanes(s, h, cw)], preferred_element_type=F32)

    def user_dot(layer, s, acc):
        return acc + nt_dot(eig[layer, s], a_ref[:, seg_lanes(s)])

    def d_copy(layer, q):
        return remote(part.at[layer, 2 * q + 1 - core], d_in.at[layer, q], RS_D + 4 * layer + q, row=partner)

    def users_reduce_out(layer, acc):
        for c in range(COLS):
            pu[layer, c] = acc[:, c * ush:(c + 1) * ush]
        for k in range(1, COLS):
            peer = lax.rem(col + k, COLS)
            send(pu.at[layer, peer], pu_in.at[layer, k], ZRS + 3 * layer + k - 1, col=peer)

    def users_reduce_in(layer):
        for k in range(1, COLS):
            arrived(pu_in.at[layer, k], ZRS + 3 * layer + k - 1)
        total = pu[layer, col] + pu_in[layer, 1] + pu_in[layer, 2] + pu_in[layer, 3]
        cur = total.astype(BF16)
        tot_u[...] = tot_u[...] + cur.astype(F32)
        if layer + 1 < LAYERS:
            eug[layer + 1, col] = cur
            users_out(layer + 1, eug.at[layer + 1, col])

    lo, hi = pl.ds(0, half), pl.ds(half, half)

    def combine(layer, q):
        s = 2 * q + core
        remote(d_in.at[layer, q], d_in.at[layer, q], RS_D + 4 * layer + q, row=row).wait_recv()
        part[layer, s] = part[layer, s] + d_in[layer, q]

    def plane_first(layer):
        base = RS_1 + 4 * layer
        combine(layer, dq)
        s = d_row
        send(part.at[layer, s, lo], r1_in.at[layer, 0], base, row=x_row)
        send(part.at[layer, s, hi], r1_in.at[layer, 2], base + 2, row=y_row)
        combine(layer, xq)
        send(part.at[layer, x_row, lo], r1_in.at[layer, 1], base + 1, row=x_row)
        combine(layer, yq)
        send(part.at[layer, y_row, hi], r1_in.at[layer, 3], base + 3, row=y_row)
        combine(layer, quad)

    def plane_second(layer):
        base = RS_1 + 4 * layer
        arrived(r1_in.at[layer, 0], base)
        part[layer, y_row, lo] = part[layer, y_row, lo] + r1_in[layer, 0]
        send(part.at[layer, y_row, lo], r2_in.at[layer, 0], RS_2 + 2 * layer, row=y_row)
        arrived(r1_in.at[layer, 2], base + 2)
        part[layer, x_row, hi] = part[layer, x_row, hi] + r1_in[layer, 2]
        send(part.at[layer, x_row, hi], r2_in.at[layer, 1], RS_2 + 2 * layer + 1, row=x_row)

    def plane_last(layer):
        base = RS_1 + 4 * layer
        arrived(r1_in.at[layer, 1], base + 1)
        arrived(r1_in.at[layer, 3], base + 3)
        arrived(r2_in.at[layer, 0], RS_2 + 2 * layer)
        arrived(r2_in.at[layer, 1], RS_2 + 2 * layer + 1)
        low = part[layer, row, lo] + r1_in[layer, 1] + r2_in[layer, 0]
        high = part[layer, row, hi] + r1_in[layer, 3] + r2_in[layer, 1]
        cur = jnp.concatenate([low, high], axis=0).astype(BF16)
        tot_i[...] = tot_i[...] + cur.astype(F32)
        if layer + 1 < LAYERS:
            eig[layer + 1, row] = cur
            items_out(layer + 1, eig.at[layer + 1, row])

    def item_product(layer):
        eu_all = users_all(layer)

        def other(q, carry):
            item_dot(layer, 2 * q + 1 - core, eu_all)
            d_copy(layer, q).start()
            return carry

        def own(q, carry):
            item_dot(layer, 2 * q + core, eu_all)
            return carry

        lax.fori_loop(0, 4, other, 0)
        lax.fori_loop(0, 4, own, 0)

    def user_product(layer):
        return lax.fori_loop(0, ROWS, lambda s, acc: user_dot(layer, s, acc), jnp.zeros((emb, users), F32))

    def normalize(s):
        for h in range(4):
            inv = deg_inv[pl.ds(4 * s + h, 1), :]

            def strip(t, carry):
                rows = pl.ds(pl.multiple_of(t * STRIP, STRIP), STRIP)
                wide = jnp.concatenate([su_ref[rows, :]] * (dw // 128), axis=1)
                cols = pl.ds(pl.multiple_of(s * seg + h * dw, 128), dw)
                a_ref[rows, cols] = a_ref[rows, cols] * (wide * inv).astype(BF16)
                return carry

            lax.fori_loop(0, users // STRIP, strip, 0)

    eu_first = users_all(0)

    def first_other(q, acc):
        s = 2 * q + 1 - core
        normalize(s)
        item_dot(0, s, eu_first)
        d_copy(0, q).start()
        return user_dot(0, s, acc)

    def first_own(q, acc):
        s = 2 * q + core
        normalize(s)
        item_dot(0, s, eu_first)
        return user_dot(0, s, acc)

    tot_u[...] = eu_ref[...].astype(F32)
    tot_i[...] = ei_ref[...].astype(F32)
    acc = lax.fori_loop(0, 4, first_other, jnp.zeros((emb, users), F32))
    acc = lax.fori_loop(0, 4, first_own, acc)
    users_reduce_out(0, acc)
    plane_first(0)
    users_reduce_in(0)
    plane_second(0)
    users_in(1)
    item_product(1)
    plane_last(0)
    plane_first(1)
    items_forward(1)
    items_in(1)
    users_reduce_out(1, user_product(1))
    plane_second(1)
    users_reduce_in(1)
    plane_last(1)
    users_in(2)
    item_product(2)
    plane_first(2)
    items_forward(2)
    items_in(2)
    users_reduce_out(2, user_product(2))
    plane_second(2)
    users_reduce_in(2)
    scale = 1.0 / (LAYERS + 1)
    out_user = (tot_u[...] * scale).astype(BF16)
    outu_ref[...] = out_user
    u_rows[row, col] = out_user
    for k in range(1, COLS):
        send(u_rows.at[row, col], u_rows.at[row, col], OUZ + k - 1, col=lax.rem(col + k, COLS))
    for k in range(1, COLS):
        arrived(u_rows.at[row, 0], OUZ + k - 1)
    for k in range(1, ROWS):
        send(u_rows.at[row], u_rows.at[row], OUR + k - 1, row=lax.rem(row + k, ROWS))
    for k in range(1, ROWS):
        arrived(u_rows.at[0], OUR + k - 1)

    n_chunks = ids_ref.shape[0] // 3
    tw = ids_ref.shape[1]

    def one_hot(ids):
        low_bits = lax.rem(ids, 128)
        same = lax.broadcasted_iota(jnp.int32, (128, tw), 0) == low_bits
        return jnp.where(same, 1.0, 0.0).astype(BF16)

    def pick(table, count, ids, first):
        hot = one_hot(ids)
        high_bits = ids // 128 - first
        acc = jnp.zeros((emb, tw), F32)
        step = min(8, count)
        for b in range(count // step):
            got = jnp.dot(table(b), hot, preferred_element_type=F32)
            for i in range(step):
                acc = acc + jnp.where(high_bits == b * step + i, got[i * emb:(i + 1) * emb, :], 0.0)
        return acc

    def pick_users(ch, carry):
        ids = ids_ref[pl.ds(ch, 1), :]
        table = lambda b: u_rows[2 * b:2 * b + 2].reshape(8 * emb, 128)
        ug[ch] = pick(table, ROWS * COLS, ids, 0)
        return carry

    lax.fori_loop(0, n_chunks, pick_users, 0)
    plane_last(2)
    out_item = (tot_i[...] * scale).astype(BF16)
    outi_ref[...] = out_item
    n_lo = seg // 128
    for b in range(n_lo):
        items_lo[b] = out_item[:, b * 128:(b + 1) * 128]
    first = (col * ROWS + row) * n_lo

    def score(ch, carry):
        pos = ids_ref[pl.ds(n_chunks + ch, 1), :]
        neg = ids_ref[pl.ds(2 * n_chunks + ch, 1), :]
        table = lambda b: items_lo[8 * b:8 * b + 8].reshape(min(8, n_lo) * emb, 128)
        vec = ug[ch]
        up = jnp.sum(vec * pick(table, n_lo, pos, first), axis=0, keepdims=True)
        down = jnp.sum(vec * pick(table, n_lo, neg, first), axis=0, keepdims=True)
        mg[pl.ds(ch, 1), :] = up - down
        return carry

    lax.fori_loop(0, n_chunks, score, 0)
    for k in range(1, COLS):
        send(mg, mg_z.at[k], MGZ + k - 1, col=lax.rem(col + k, COLS))
    for k in range(1, COLS):
        arrived(mg_z.at[k], MGZ + k - 1)
    mg_zsum[...] = mg[...] + mg_z[1] + mg_z[2] + mg_z[3]
    for k in range(1, ROWS):
        send(mg_zsum, mg_r.at[k], MGR + k - 1, row=lax.rem(row + k, ROWS))
    for k in range(1, ROWS):
        arrived(mg_r.at[k], MGR + k - 1)
    margin = mg_zsum[...]
    for k in range(1, ROWS):
        margin = margin + mg_r[k]
    margin_ref[...] = margin

    for layer in range(LAYERS):
        for q in range(4):
            d_copy(layer, q).wait_send()
    for copy in sent:
        copy.wait_send()


def solution(mesh):
    def device_body(mask_blk, user_shard, item_shard, triples):
        users, block = mask_blk.shape
        emb = user_shard.shape[1]
        ush, seg = user_shard.shape[0], item_shard.shape[0]
        batch = triples.shape[0]
        tw = batch // 8
        dw = block // 32
        ids = triples.T.reshape(3 * 8, tw)
        vmem = pl.BlockSpec(memory_space=pltpu.VMEM)
        out_u, out_i, margin = pl.pallas_call(
            kernel,
            out_shape=(
                jax.ShapeDtypeStruct((emb, ush), BF16),
                jax.ShapeDtypeStruct((emb, seg), BF16),
                jax.ShapeDtypeStruct((8, tw), F32),
            ),
            in_specs=[pl.BlockSpec(memory_space=pl.ANY), vmem, vmem, vmem],
            out_specs=(vmem, vmem, vmem),
            scratch_shapes=[
                pltpu.VMEM((users, block), BF16),
                pltpu.VMEM((SLOTS, users, block // CHUNKS), jnp.int32),
                pltpu.VMEM((32, dw), F32),
                pltpu.VMEM((ROWS, 32, dw), F32),
                pltpu.VMEM((32, dw), F32),
                pltpu.VMEM((users, 128), F32),
                pltpu.VMEM((8, users), F32),
                pltpu.VMEM((COLS, 8, users), F32),
                pltpu.VMEM((users, 128), F32),
                pltpu.VMEM((LAYERS, ROWS, emb, seg), F32),
                pltpu.VMEM((LAYERS, 4, emb, seg), F32),
                pltpu.VMEM((LAYERS, 4, emb // 2, seg), F32),
                pltpu.VMEM((LAYERS, 2, emb // 2, seg), F32),
                pltpu.VMEM((LAYERS, ROWS, emb, seg), BF16),
                pltpu.VMEM((LAYERS, COLS, emb, ush), BF16),
                pltpu.VMEM((LAYERS, COLS, emb, ush), F32),
                pltpu.VMEM((LAYERS, COLS, emb, ush), F32),
                pltpu.VMEM((emb, seg), F32),
                pltpu.VMEM((emb, ush), F32),
                pltpu.VMEM((seg // 128, emb, 128), BF16),
                pltpu.VMEM((8, emb, tw), F32),
                pltpu.VMEM((ROWS, COLS, emb, ush), BF16),
                pltpu.VMEM((8, tw), F32),
                pltpu.VMEM((COLS, 8, tw), F32),
                pltpu.VMEM((8, tw), F32),
                pltpu.VMEM((ROWS, 8, tw), F32),
                pltpu.SemaphoreType.DMA((SLOTS,)),
                pltpu.SemaphoreType.DMA((N_SEM,)),
                pltpu.SemaphoreType.DMA((N_SEM,)),
            ],
            compiler_params=pltpu.CompilerParams(
                collective_id=0, has_side_effects=True, vmem_limit_bytes=62 * 1024 * 1024),
        )(mask_blk, user_shard.T, item_shard.T, ids)
        return out_u.T, out_i.T, jax.nn.softplus(-margin.reshape(batch))

    return jax.shard_map(
        device_body,
        mesh=mesh,
        in_specs=(P("row", "col"), P(("row", "col"), None), P(("col", "row"), None), P()),
        out_specs=(P(("row", "col"), None), P(("col", "row"), None), P()),
        check_vma=False,
    )
```

time: 526 us -> 119 us (0.23)
  waiting for transfers between devices: 305 us -> 0 us
  Pallas kernels: 0 us -> 112 us
  matrix products: 59.8 us -> 0 us
  blocking collectives: 49.4 us -> 0 us
  local copies, waits for them, and re-layouts: 50.3 us -> 4.37 us
  other arithmetic: 45.9 us -> 1.35 us
  between operations: 14 us -> 0.64 us
    psum x2 -> x0, waiting for transfers between devices: 162 us -> none  [the longest x1 130 us: device_body(): picked = lax.psum(picked, ('row', 'col'))]
    reduce_scatter x6 -> x0, waiting for transfers between devices: 132 us -> none  [the longest x3 95.2 us: device_body(): lax.psum_scatter(item_part, 'row', scatter_dimension=0, tiled=True)]
    pallas_call x0 -> x1, Pallas kernels: none -> 112 us  [device_body(): pl.pallas_call(kernel, out_shape=(jax.ShapeDtypeStruct((emb, ush), BF16),...]
    dot_general x6 -> x0, matrix products: 59.8 us -> none  [the longest x3 35.2 us: device_body(): jnp.dot(adj_norm, item_panel, preferred_element_type=jnp.float32)]
    all_gather x3 -> x0, blocking collectives: 39.4 us -> none  [device_body(): user_panel = lax.all_gather(cur_user, 'col', axis=0, tiled=True)]
    gather x3 -> x0, local copies, waits for them, and re-layouts: 39.2 us -> none  [lookup(): jnp.take(emb_table, jnp.clip(local_ids, 0, emb_table.shape[0] - 1), axis=0)]
    convert_element_type x6 -> x0, other arithmetic: 18.6 us -> none  [the longest x1 13.1 us: device_body(): (mask_blk.astype(jnp.float32) * scale_user[:, None] * scale_item[None, :]...]
    reduce_sum x2 -> x0, other arithmetic: 14.6 us -> none  [the longest x1 13.1 us: device_body(): deg_user = lax.psum(jnp.sum(mask_blk, axis=1), 'col')]
  transfers between devices with their start and end apart: 11 -> 0, of which waited for: 10 -> 0; matrix products, arithmetic and copies ran while one was open for 18% -> 0% of each run, Pallas kernels for 0% -> 0%
where the time goes in v1:
time: 119 us
  Pallas kernels  112 us (94%)
  local copies, waits for them, and re-layouts  4.37 us (4%)
  other arithmetic  1.35 us (1%)
    pallas_call x1, Pallas kernels, device_body(): pl.pallas_call(kernel, out_shape=(jax.ShapeDtypeStruct((emb, ush), BF16),...  112 us
    unnamed x3, local copies, waits for them, and re-layouts  2.87 us

profile of v1, /device:TPU:0, one launch (start us, length us, event | category | flops | bytes accessed | tf_op | source)
XLA Modules:
  0.0 118.8 jit_solution(4721232826071149860)
XLA Ops:
  0.6 1.5 %reshape.11.ids_ref = s32[24,512]{1,0:T(8,128)} reshape(s32[3,4096]{1,0:T(4,128)} %bitcast.10) | data formatting | bytes 98304 | tf_op jit(solution)/shard_map/reshape | solution.py:402
  2.1 112.5 %shard_map.67 = (bf16[32,128]{1,0:T(8,128)(2,1)}, bf16[32,2048]{1,0:T(8,128)(2,1)}, f32[8,512]{1,0:T(8,128)}) custom-call(s32[512,16384]{1,0:T(8,128)} %mask_hbm.1, bf16[32,128]{1,0:T(8,128)(2,1)} %bitcast.12, bf16[32,2048]{1,0:T(8,128)(2,1)} %bitcast.8, s32[24,512]{1,0:T(8,128)} %reshape.11.ids_ref), custom_call_target="tpu_custom_call" | custom-call | tf_op jit(solution)/shard_map/pallas_call | solution.py:404
  114.6 0.7 negate_bitcast_fusion
  115.3 0.6 compare_select_fusion
  116.0 1.3 %copy.10 = bf16[128,32]{0,1:T(8,128)(2,1)} copy(bf16[128,32]{0,1:T(8,128)(2,1)} %bitcast.13) | data formatting | bytes 16384
  117.3 1.6 %copy.11 = bf16[2048,32]{0,1:T(8,128)(2,1)} copy(bf16[2048,32]{0,1:T(8,128)(2,1)} %bitcast.9) | data formatting | bytes 262144
  (1 shorter events, 0.0 us)

commit v2 on v1

v2 whole, which is shorter than its diff:
```python
import functools

import jax
import jax.numpy as jnp
from jax import lax
from jax.experimental import pallas as pl
from jax.experimental.pallas import tpu as pltpu
from jax.sharding import PartitionSpec as P

LAYERS = 3
ROWS = 8
COLS = 4
SLOTS = 4
CHUNKS = 16
STRIP = 32
MESH_ID = pl.DeviceIdType.MESH
F32 = jnp.float32
BF16 = jnp.bfloat16

DEG = 0
UDEG = 28
AG = 31
ZAG = AG + 21
ZRS = ZAG + 9
RS_D = ZRS + 9
RS_1 = RS_D + 12
RS_2 = RS_1 + 12
OUZ = RS_2 + 6
OUR = OUZ + 3
MGZ = OUR + 7
MGR = MGZ + 3
N_SEM = MGR + 7


def nt_dot(a, b):
    return lax.dot_general(a, b, (((1,), (1,)), ((), ())), preferred_element_type=F32)


def kernel(mask_hbm, eu_hbm, ei_hbm, ids_hbm, outu_hbm, outi_hbm, loss_hbm,
           a_ref, mbuf, deg_own, deg_in, deg_inv, udeg_part, udeg_own, udeg_in, su_ref,
           part, d_in, r1_in, r2_in, eig, eug, pu, pu_in, tot_i, tot_u,
           items_lo, up_rows, down_rows, u_rows, mg, mg_z, mg_zsum, mg_r, ids_ref, outi_ref,
           copy_sem, in_sem, send_sem, recv_sem):
    emb, seg = tot_i.shape
    users, block = a_ref.shape
    ush = tot_u.shape[1]
    cw = block // CHUNKS
    dw = block // 32
    row = lax.axis_index("row")
    col = lax.axis_index("col")
    core = lax.rem(row, 2)
    quad = row // 2
    partner = row + 1 - 2 * core
    at_x, at_y = lax.rem(quad, 2), quad // 2
    half = emb // 2
    sent = []

    def flipped(j):
        fx, fy = lax.rem(j, 2), j // 2
        return (at_y + fy - 2 * at_y * fy) * 2 + at_x + fx - 2 * at_x * fx

    x_row, y_row = 2 * flipped(1) + core, 2 * flipped(2) + core

    def remote(src, dst, idx, **where):
        return pltpu.make_async_remote_copy(
            src_ref=src, dst_ref=dst, send_sem=send_sem.at[idx], recv_sem=recv_sem.at[idx],
            device_id=where, device_id_type=MESH_ID)

    def send(src, dst, idx, **where):
        copy = remote(src, dst, idx, **where)
        copy.start()
        sent.append(copy)

    def arrived(dst, idx):
        remote(dst, dst, idx, row=row).wait_recv()

    def mask_copy(j):
        return pltpu.make_async_copy(
            mask_hbm.at[:, pl.ds(j * cw, cw)], mbuf.at[j % SLOTS], copy_sem.at[j % SLOTS])

    small = [
        pltpu.make_async_copy(eu_hbm, eug.at[0, col], in_sem.at[0]),
        pltpu.make_async_copy(ei_hbm, eig.at[0, row], in_sem.at[1]),
        pltpu.make_async_copy(ids_hbm, ids_ref, in_sem.at[2]),
    ]
    small[0].start()
    small[1].start()
    for j in range(SLOTS):
        mask_copy(j).start()
    small[2].start()

    barrier = pltpu.get_barrier_semaphore()
    for k in range(1, ROWS):
        pl.semaphore_signal(barrier, inc=1, device_id={"row": lax.rem(row + k, ROWS)}, device_id_type=MESH_ID)
    for k in range(1, COLS):
        pl.semaphore_signal(barrier, inc=1, device_id={"col": lax.rem(col + k, COLS)}, device_id_type=MESH_ID)
    pl.semaphore_wait(barrier, ROWS + COLS - 2)

    def items_out(layer):
        src = eig.at[layer, row]
        for j in range(1, 4):
            send(src, src, AG + 7 * layer + j - 1, row=2 * flipped(j) + core)
        send(src, src, AG + 7 * layer + 3, row=partner)

    def items_from(layer, j):
        ref = eig.at[layer, 2 * flipped(j) + core]
        arrived(ref, AG + 7 * layer + j - 1)
        remote(ref, ref, AG + 7 * layer + 3 + j, row=partner).start()

    def items_from_partner(layer, j):
        arrived(eig.at[layer, 2 * flipped(j) + 1 - core], AG + 7 * layer + 3 + j)

    def users_out(layer):
        src = eug.at[layer, col]
        for k in range(1, COLS):
            send(src, src, ZAG + 3 * layer + k - 1, col=lax.rem(col + k, COLS))

    def users_in(layer):
        for k in range(COLS - 1):
            arrived(eug.at[layer, 0], ZAG + 3 * layer + k)

    small[0].wait()
    users_out(0)
    small[1].wait()
    items_out(0)
    small[2].wait()

    udeg_part[...] = jnp.zeros_like(udeg_part)
    for j in range(CHUNKS):
        mask_copy(j).wait()

        def strip(s, acc, j=j):
            rows = pl.ds(pl.multiple_of(s * STRIP, STRIP), STRIP)
            m = mbuf[j % SLOTS, rows, :].astype(F32)
            a_ref[rows, j * cw:(j + 1) * cw] = m.astype(BF16)
            lanes = m[:, 0:128]
            for t in range(1, cw // 128):
                lanes = lanes + m[:, t * 128:(t + 1) * 128]
            udeg_part[rows, :] = udeg_part[rows, :] + lanes
            for t in range(STRIP // 8):
                acc = acc + m[t * 8:(t + 1) * 8, :]
            return acc

        acc = lax.fori_loop(0, users // STRIP, strip, jnp.zeros((8, cw), F32))
        if j + SLOTS < CHUNKS:
            mask_copy(j + SLOTS).start()
        total = jnp.sum(acc, axis=0, keepdims=True)
        deg_own[2 * j:2 * j + 1, :] = total[:, :dw]
        deg_own[2 * j + 1:2 * j + 2, :] = total[:, dw:]
        if j % 4 == 3:
            g = j // 4
            for k in range(1, ROWS):
                send(deg_own.at[pl.ds(8 * g, 8), :], deg_in.at[k, pl.ds(8 * g, 8), :],
                     DEG + 7 * g + k - 1, row=lax.rem(row + k, ROWS))
        if j == 7:
            for k in range(1, 4):
                items_from(0, k)

    udeg_own[...] = nt_dot(jnp.ones((8, 128), BF16), udeg_part[...].astype(BF16))
    for k in range(1, COLS):
        send(udeg_own, udeg_in.at[k], UDEG + k - 1, col=lax.rem(col + k, COLS))
    tot_u[...] = eug[0, col].astype(F32)
    tot_i[...] = eig[0, row].astype(F32)
    users_in(0)
    for k in range(4):
        items_from_partner(0, k)
    for k in range(1, COLS):
        arrived(udeg_in.at[k], UDEG + k - 1)
    du = udeg_own[...] + udeg_in[1] + udeg_in[2] + udeg_in[3]
    su = lax.rsqrt(jnp.maximum(du, 1.0))
    for b in range(users // 128):
        wide = jnp.broadcast_to(su[0:1, b * 128:(b + 1) * 128], (128, 128))
        su_ref[b * 128:(b + 1) * 128, :] = wide.T
    for g in range(4):
        for k in range(1, ROWS):
            arrived(deg_in.at[k, pl.ds(8 * g, 8), :], DEG + 7 * g + k - 1)
    di = deg_own[...]
    for k in range(1, ROWS):
        di = di + deg_in[k]
    deg_inv[...] = lax.rsqrt(jnp.maximum(di, 1.0))

    def users_all(layer):
        return jnp.concatenate([eug[layer, c] for c in range(COLS)], axis=1)

    def seg_lanes(s, start=0, width=seg):
        return pl.ds(pl.multiple_of(s * seg + start, 128), width)

    def item_dot(layer, s, eu_all):
        for h in range(2):
            part[layer, s, :, h * cw:(h + 1) * cw] = jnp.dot(
                eu_all, a_ref[:, seg_lanes(s, h * cw, cw)], preferred_element_type=F32)

    def user_dot(layer, s, acc):
        return acc + nt_dot(eig[layer, s], a_ref[:, seg_lanes(s)])

    lo, hi = pl.ds(0, half), pl.ds(half, half)

    def d_copy(layer, i, s):
        return remote(part.at[layer, s], d_in.at[layer, i], RS_D + 4 * layer + i, row=partner)

    def x_first(layer, i, s):
        return remote(part.at[layer, s, lo], r1_in.at[layer, i // 2], RS_1 + 4 * layer + i // 2, row=x_row)

    def y_first(layer, i, s):
        return remote(part.at[layer, s, hi], r1_in.at[layer, 2 + i], RS_1 + 4 * layer + 2 + i, row=y_row)

    def plane_start(layer, i, s):
        arrived(d_in.at[layer, i], RS_D + 4 * layer + i)
        part[layer, s] = part[layer, s] + d_in[layer, i]

        @pl.when(jnp.logical_or(i == 0, i == 2))
        def _():
            x_first(layer, i, s).start()

        @pl.when(i < 2)
        def _():
            y_first(layer, i, s).start()

    def item_product(layer):
        eu_all = users_all(layer)

        def other(i, carry):
            s = 2 * flipped(3 - i) + 1 - core
            item_dot(layer, s, eu_all)
            d_copy(layer, i, s).start()
            return carry

        def own(i, carry):
            s = 2 * flipped(3 - i) + core
            item_dot(layer, s, eu_all)
            plane_start(layer, i, s)
            return carry

        lax.fori_loop(0, 4, other, 0)
        lax.fori_loop(0, 4, own, 0)

    def plane_second(layer):
        base = RS_1 + 4 * layer
        arrived(r1_in.at[layer, 0], base)
        part[layer, y_row, lo] = part[layer, y_row, lo] + r1_in[layer, 0]
        send(part.at[layer, y_row, lo], r2_in.at[layer, 0], RS_2 + 2 * layer, row=y_row)
        arrived(r1_in.at[layer, 2], base + 2)
        part[layer, x_row, hi] = part[layer, x_row, hi] + r1_in[layer, 2]
        send(part.at[layer, x_row, hi], r2_in.at[layer, 1], RS_2 + 2 * layer + 1, row=x_row)

    def plane_last(layer):
        base = RS_1 + 4 * layer
        arrived(r1_in.at[layer, 1], base + 1)
        arrived(r1_in.at[layer, 3], base + 3)
        arrived(r2_in.at[layer, 0], RS_2 + 2 * layer)
        arrived(r2_in.at[layer, 1], RS_2 + 2 * layer + 1)
        low = part[layer, row, lo] + r1_in[layer, 1] + r2_in[layer, 0]
        high = part[layer, row, hi] + r1_in[layer, 3] + r2_in[layer, 1]
        cur = jnp.concatenate([low, high], axis=0).astype(BF16)
        if layer + 1 < LAYERS:
            eig[layer + 1, row] = cur
            items_out(layer + 1)
        tot_i[...] = tot_i[...] + cur.astype(F32)

    def user_product(layer):
        def chip(j, acc):
            @pl.when(j > 0)
            def _():
                items_from(layer, j)

            acc = user_dot(layer, 2 * flipped(j) + core, acc)
            items_from_partner(layer, j)
            return user_dot(layer, 2 * flipped(j) + 1 - core, acc)

        return lax.fori_loop(0, 4, chip, jnp.zeros((emb, users), F32))

    def users_reduce_out(layer, acc):
        for c in range(COLS):
            pu[layer, c] = acc[:, c * ush:(c + 1) * ush]
        for k in range(1, COLS):
            peer = lax.rem(col + k, COLS)
            send(pu.at[layer, peer], pu_in.at[layer, k], ZRS + 3 * layer + k - 1, col=peer)

    def users_reduce_in(layer):
        for k in range(1, COLS):
            arrived(pu_in.at[layer, k], ZRS + 3 * layer + k - 1)
        total = pu[layer, col] + pu_in[layer, 1] + pu_in[layer, 2] + pu_in[layer, 3]
        cur = total.astype(BF16)
        if layer + 1 < LAYERS:
            eug[layer + 1, col] = cur
            users_out(layer + 1)
        tot_u[...] = tot_u[...] + cur.astype(F32)

    tile = 256
    eu_first = users_all(0)
    n_u = users // tile

    def first_segment(s, acc):
        acc = list(acc)
        for h in range(seg // tile):
            cols = seg_lanes(s, h * tile, tile)
            start = h * tile
            inv = deg_inv[pl.ds(s * (seg // dw) + start // dw, 1), start % dw:start % dw + tile]
            items = eig[0, s, :, start:start + tile]
            got = None
            for u in range(n_u):
                rows = slice(u * tile, (u + 1) * tile)
                wide = jnp.concatenate([su_ref[rows, :]] * (tile // 128), axis=1)
                block_a = a_ref[rows, cols] * (wide * inv).astype(BF16)
                a_ref[rows, cols] = block_a
                more = jnp.dot(eu_first[:, rows], block_a, preferred_element_type=F32)
                got = more if got is None else got + more
                acc[u] = acc[u] + nt_dot(items, block_a)
            part[0, s, :, start:start + tile] = got
        return tuple(acc)

    def first_other(i, acc):
        s = 2 * flipped(3 - i) + 1 - core
        acc = first_segment(s, acc)
        d_copy(0, i, s).start()
        return acc

    def first_own(i, acc):
        s = 2 * flipped(3 - i) + core
        acc = first_segment(s, acc)
        plane_start(0, i, s)
        return acc

    acc = tuple(jnp.zeros((emb, tile), F32) for _ in range(n_u))
    acc = lax.fori_loop(0, 4, first_other, acc)
    acc = lax.fori_loop(0, 4, first_own, acc)
    users_reduce_out(0, jnp.concatenate(acc, axis=1))
    plane_second(0)
    users_reduce_in(0)
    plane_last(0)
    users_in(1)
    item_product(1)
    users_reduce_out(1, user_product(1))
    plane_second(1)
    users_reduce_in(1)
    plane_last(1)
    users_in(2)
    item_product(2)
    users_reduce_out(2, user_product(2))
    plane_second(2)
    users_reduce_in(2)
    scale = 1.0 / (LAYERS + 1)
    u_rows[row, col] = (tot_u[...] * scale).astype(BF16)
    for k in range(1, COLS):
        send(u_rows.at[row, col], u_rows.at[row, col], OUZ + k - 1, col=lax.rem(col + k, COLS))
    out_copy = [pltpu.make_async_copy(u_rows.at[row, col], outu_hbm, in_sem.at[0])]
    out_copy[0].start()

    n_chunks = up_rows.shape[0]
    tw = up_rows.shape[2]

    def one_hot(ids):
        low_bits = lax.rem(ids, 128)
        same = lax.broadcasted_iota(jnp.int32, (128, tw), 0) == low_bits
        return jnp.where(same, 1.0, 0.0).astype(BF16)

    def pick(table, count, ids, first):
        hot = one_hot(ids)
        high_bits = ids // 128 - first
        acc = jnp.zeros((emb, tw), F32)
        step = min(8, count)
        for b in range(count // step):
            got = jnp.dot(table(b), hot, preferred_element_type=F32)
            for i in range(step):
                acc = acc + jnp.where(high_bits == b * step + i, got[i * emb:(i + 1) * emb, :], 0.0)
        return acc

    def ids_of(which, ch):
        return ids_ref[which:which + 1, pl.ds(pl.multiple_of(ch * tw, 128), tw)]

    plane_last(2)
    out_item = (tot_i[...] * scale).astype(BF16)
    outi_ref[...] = out_item
    out_copy.append(pltpu.make_async_copy(outi_ref, outi_hbm, in_sem.at[1]))
    out_copy[1].start()
    n_lo = seg // 128
    for b in range(n_lo):
        items_lo[b] = out_item[:, b * 128:(b + 1) * 128]
    first = (col * ROWS + row) * n_lo

    for k in range(1, COLS):
        arrived(u_rows.at[row, 0], OUZ + k - 1)
    for k in range(1, ROWS):
        send(u_rows.at[row], u_rows.at[row], OUR + k - 1, row=lax.rem(row + k, ROWS))

    def pick_items(ch, carry):
        table = lambda b: items_lo[8 * b:8 * b + 8].reshape(min(8, n_lo) * emb, 128)
        up_rows[ch] = pick(table, n_lo, ids_of(1, ch), first)
        down_rows[ch] = pick(table, n_lo, ids_of(2, ch), first)
        return carry

    lax.fori_loop(0, n_chunks, pick_items, 0)
    for k in range(1, ROWS):
        arrived(u_rows.at[0], OUR + k - 1)

    def score(ch, carry):
        table = lambda b: u_rows[2 * b:2 * b + 2].reshape(8 * emb, 128)
        vec = pick(table, ROWS * COLS, ids_of(0, ch), 0)
        up = jnp.sum(vec * up_rows[ch], axis=0, keepdims=True)
        down = jnp.sum(vec * down_rows[ch], axis=0, keepdims=True)
        diff = up - down
        for t in range(tw // 128):
            mg[pl.ds(ch * (tw // 128) + t, 1), :] = diff[:, t * 128:(t + 1) * 128]
        return carry

    lax.fori_loop(0, n_chunks, score, 0)
    for k in range(1, COLS):
        send(mg, mg_z.at[k], MGZ + k - 1, col=lax.rem(col + k, COLS))
    for k in range(1, COLS):
        arrived(mg_z.at[k], MGZ + k - 1)
    mg_zsum[...] = mg[...] + mg_z[1] + mg_z[2] + mg_z[3]
    for k in range(1, ROWS):
        send(mg_zsum, mg_r.at[k], MGR + k - 1, row=lax.rem(row + k, ROWS))
    for k in range(1, ROWS):
        arrived(mg_r.at[k], MGR + k - 1)
    margin = mg_zsum[...]
    for k in range(1, ROWS):
        margin = margin + mg_r[k]
    mg_z[0] = jnp.maximum(-margin, 0.0) + jnp.log1p(jnp.exp(-jnp.abs(margin)))
    out_copy.append(pltpu.make_async_copy(mg_z.at[0], loss_hbm, in_sem.at[2]))
    out_copy[2].start()

    for layer in range(LAYERS):
        for i in range(4):
            d_copy(layer, i, row).wait_send()
        for i in range(2):
            x_first(layer, 2 * i, row).wait_send()
            y_first(layer, i, row).wait_send()
        for j in range(1, 4):
            ref = eig.at[layer, row]
            remote(ref, ref, AG + 7 * layer + 3 + j, row=partner).wait_send()
    for copy in sent:
        copy.wait_send()
    for copy in out_copy:
        copy.wait()


def solution(mesh):
    def device_body(mask_blk, user_shard, item_shard, triples):
        users, block = mask_blk.shape
        emb = user_shard.shape[1]
        ush, seg = user_shard.shape[0], item_shard.shape[0]
        batch = triples.shape[0]
        tw = batch // 8
        dw = block // 32
        hbm = pl.BlockSpec(memory_space=pl.ANY)
        loss_shape = (batch // 128, 128)
        out_u, out_i, loss = pl.pallas_call(
            kernel,
            out_shape=(
                jax.ShapeDtypeStruct((emb, ush), BF16),
                jax.ShapeDtypeStruct((emb, seg), BF16),
                jax.ShapeDtypeStruct(loss_shape, F32),
            ),
            in_specs=[pl.BlockSpec(memory_space=pltpu.HBM)] * 4,
            out_specs=(hbm,) * 3,
            scratch_shapes=[
                pltpu.VMEM((users, block), BF16),
                pltpu.VMEM((SLOTS, users, block // CHUNKS), jnp.int32),
                pltpu.VMEM((32, dw), F32),
                pltpu.VMEM((ROWS, 32, dw), F32),
                pltpu.VMEM((32, dw), F32),
                pltpu.VMEM((users, 128), F32),
                pltpu.VMEM((8, users), F32),
                pltpu.VMEM((COLS, 8, users), F32),
                pltpu.VMEM((users, 128), F32),
                pltpu.VMEM((LAYERS, ROWS, emb, seg), F32),
                pltpu.VMEM((LAYERS, 4, emb, seg), F32),
                pltpu.VMEM((LAYERS, 4, emb // 2, seg), F32),
                pltpu.VMEM((LAYERS, 2, emb // 2, seg), F32),
                pltpu.VMEM((LAYERS, ROWS, emb, seg), BF16),
                pltpu.VMEM((LAYERS, COLS, emb, ush), BF16),
                pltpu.VMEM((LAYERS, COLS, emb, ush), F32),
                pltpu.VMEM((LAYERS, COLS, emb, ush), F32),
                pltpu.VMEM((emb, seg), F32),
                pltpu.VMEM((emb, ush), F32),
                pltpu.VMEM((seg // 128, emb, 128), BF16),
                pltpu.VMEM((8, emb, tw), F32),
                pltpu.VMEM((8, emb, tw), F32),
                pltpu.VMEM((ROWS, COLS, emb, ush), BF16),
                pltpu.VMEM(loss_shape, F32),
                pltpu.VMEM((COLS,) + loss_shape, F32),
                pltpu.VMEM(loss_shape, F32),
                pltpu.VMEM((ROWS,) + loss_shape, F32),
                pltpu.VMEM((3, batch), jnp.int32),
                pltpu.VMEM((emb, seg), BF16),
                pltpu.SemaphoreType.DMA((SLOTS,)),
                pltpu.SemaphoreType.DMA((3,)),
                pltpu.SemaphoreType.DMA((N_SEM,)),
                pltpu.SemaphoreType.DMA((N_SEM,)),
            ],
            compiler_params=pltpu.CompilerParams(
                collective_id=0, has_side_effects=True, vmem_limit_bytes=48 * 1024 * 1024),
        )(mask_blk, user_shard.T, item_shard.T, triples.T)
        return out_u.T, out_i.T, loss.reshape(batch)

    return jax.shard_map(
        device_body,
        mesh=mesh,
        in_specs=(P("row", "col"), P(("row", "col"), None), P(("col", "row"), None), P()),
        out_specs=(P(("row", "col"), None), P(("col", "row"), None), P()),
        check_vma=False,
    )
```

time: 119 us -> 98.7 us (0.83)
  Pallas kernels: 112 us -> 93.5 us
  other arithmetic: 1.35 us -> 0 us
    pallas_call x1, Pallas kernels: 112 us -> 93.5 us  [device_body(): pl.pallas_call(kernel, out_shape=(jax.ShapeDtypeStruct((emb, ush), BF16),...]
    reshape x1 -> x0, local copies, waits for them, and re-layouts: 1.5 us -> none  [device_body(): ids = triples.T.reshape(3 * 8, tw)]
    unnamed x3 -> x9, local copies, waits for them, and re-layouts: 2.87 us -> 4.29 us
where the time goes in v2:
time: 98.7 us; the launch traced here: 98.4 us
  Pallas kernels  93.5 us (95%)
  local copies, waits for them, and re-layouts  4.29 us (4%)
    pallas_call x1, Pallas kernels, device_body(): pl.pallas_call(kernel, out_shape=(jax.ShapeDtypeStruct((emb, ush), BF16),...  93.5 us
    unnamed x9, local copies, waits for them, and re-layouts  4.29 us

profile of v2, /device:TPU:0, one launch (start us, length us, event | category | flops | bytes accessed | tf_op | source)
XLA Modules:
  0.0 98.4 jit_solution(8485163464955791139)
XLA Ops:
  0.6 0.0 copy-start
  0.6 0.9 copy-done
  1.5 0.0 copy-start.1
  1.5 0.8 copy-done.1
  2.4 0.0 copy-start.2
  2.4 0.7 copy-done.2
  3.1 93.5 %shard_map.67 = (bf16[32,128]{1,0:T(8,128)(2,1)S(1)}, bf16[32,2048]{1,0:T(8,128)(2,1)S(1)}, f32[32,128]{1,0:T(8,128)S(1)}) custom-call(s32[512,16384]{1,0:T(8,128)} %mask_hbm.1, bf16[32,128]{1,0:T(8,128)(2,1)S(1)} %bitcast.10, bf16[32,2048]{1,0:T(8,128)(2,1)S(1)} %bitcast.6, s32[3,4096]{1,0:T(4,128)S(1)} %bitcast.8), custom_call_target="tpu_custom_call" | custom-call | tf_op jit(solution)/shard_map/pallas_call | solution.py:448
  96.6 0.6 copy.10
  97.2 0.7 copy.11
  97.8 0.6 copy.12
Async XLA Ops:
  0.6 0.9 copy-start
  1.5 0.8 copy-start.1
  2.4 0.7 copy-start.2
